TPU v7x, 64 devices: a 2x2x8 block of a 4x4x8 slice. The times are simulated.
64 devices in a mesh: dp: 4 (over x, y), dcp: 16 (over z, core).
Axes of the slice: x: 2, y: 2, z: 8, core: 2. Of those that a mesh axis runs over, the one named last changes fastest.
The devices are a block of a 4x4x8 slice.
Arguments:
- q_abs: bfloat16 [256, 64, 576], P('dp', 'dcp'), parts along dimension 0
- kv_cache: bfloat16 [256, 4, 16, 64, 576], P('dp', None, 'dcp'), parts along dimension 0
- lengths: int32 [256], P('dp'), parts along dimension 0
- w_uv: bfloat16 [64, 512, 128], replicated
Outputs:
- output: bfloat16 [256, 64, 128], P('dp', 'dcp'), parts along dimension 0
There are 4 independent parts. A program takes and returns all parts, laid end to end along the dimension named above; an argument that names none is the same for every part.
All inputs are finite; a program needn't handle non-finite values.
Results may differ from a plain program's by a relative error of at most 0.00935943.
Values are sent between devices in bfloat16 or wider.
A program may use at most 768 MiB of HBM per device.

v0:
```python
import jax
import jax.numpy as jnp
from jax import lax
from jax.sharding import PartitionSpec as P


def solution(mesh):
    group_size = mesh.shape["dcp"]

    def local_attend(q_own, kv_cache, lengths, w_uv):
        n_batch, pages_dev, _, page_len, kv_dim = kv_cache.shape
        head_loc = q_own.shape[1]
        latent = w_uv.shape[1]
        v_dim = w_uv.shape[2]
        qk_scale = (v_dim + kv_dim - latent) ** -0.5
        dev_idx = lax.axis_index("dcp")
        q_all = lax.all_gather(q_own, "dcp", axis=1, tiled=True)
        c_flat = kv_cache.reshape(n_batch, pages_dev * page_len, kv_dim)
        pos_ids = ((jnp.arange(pages_dev)[:, None] * group_size + dev_idx) * page_len + jnp.arange(page_len)[None, :]).reshape(-1)
        valid_mask = pos_ids[None, None, :] < lengths[:, None, None]
        scores = jnp.einsum("bhk,btk->bht", q_all, c_flat, preferred_element_type=jnp.float32) * qk_scale
        scores = jnp.where(valid_mask, scores, -jnp.inf)
        row_max = jnp.max(scores, axis=-1)
        exp_scores = jnp.exp(scores - row_max[..., None])
        row_sum = jnp.sum(exp_scores, axis=-1)
        o_part = jnp.einsum("bht,btl->bhl", exp_scores.astype(jnp.bfloat16), c_flat[..., :latent], preferred_element_type=jnp.float32)
        o_part = (o_part / row_sum[..., None]).astype(jnp.bfloat16)
        lse_part = row_max + jnp.log(row_sum)
        v_part = jnp.einsum("bhl,hlv->bhv", o_part, w_uv, preferred_element_type=jnp.float32).astype(jnp.bfloat16)
        v_recv = lax.all_to_all(v_part, "dcp", 1, 1, tiled=True)
        lse_recv = lax.all_to_all(lse_part, "dcp", 1, 1, tiled=True)
        v_recv = v_recv.reshape(n_batch, group_size, head_loc, v_dim)
        lse_recv = lse_recv.reshape(n_batch, group_size, head_loc)
        lse_tot = jax.nn.logsumexp(lse_recv, axis=1)
        weight = jnp.exp(lse_recv - lse_tot[:, None, :])
        out_v = jnp.sum(weight[..., None] * v_recv.astype(jnp.float32), axis=1)
        return out_v.astype(jnp.bfloat16)

    return jax.shard_map(
        local_attend,
        mesh=mesh,
        in_specs=(P("dp", "dcp", None), P("dp", None, "dcp", None, None), P("dp"), P(None, None, None)),
        out_specs=P("dp", "dcp", None),
        check_vma=False,
    )
```

profile of v0, /device:TPU:22, one launch (start us, length us, event | category | flops | bytes accessed | tf_op | source)
XLA Modules:
  0.0 138.1 jit_solution(2888917721722016538)
XLA Ops:
  6.5 0.0 all-gather.2.cloned.1.call-start
  6.6 1.7 %copy.10 = bf16[64,4,576]{2,0,1:T(8,128)(2,1)} copy(bf16[64,4,576]{2,1,0:T(4,128)(2,1)} %param.4) | data formatting | bytes 589824 | tf_op args[0]
  8.3 0.1 all-gather.2.cloned.1.call-update
  8.4 0.1 iota_add_fusion
  8.4 0.1 add.50
  8.5 0.7 broadcast_compare_fusion
  9.3 43.7 %all-gather.2.cloned.1.call-done = bf16[64,64,576]{2,0,1:T(8,128)(2,1)} async-done(((bf16[64,4,576]{2,0,1:T(8,128)(2,1)}), bf16[64,64,576]{2,0,1:T(8,128)(2,1)}) %all-gather.2.cloned.1.call-update) | async-done | bytes 4718608 | tf_op jit(solution)/shard_map/all_gather | solution.py:17
  52.9 13.3 %fusion.6 = (f32[64,64]{1,0:T(8,128)S(1)}, f32[64,64,256]{2,1,0:T(8,128)}) fusion(pred[64,256]{1,0:T(8,128)(4,1)S(1)} %broadcast_compare_fusion, bf16[64,256,576]{2,1,0:T(8,128)(2,1)} %bitcast.13, bf16[64,64,576]{2,0,1:T(8,128)(2,1)} %all-gather.2.cloned.1.call-done), kind=kOutput, calls=%fused_computation.9 | convolution fusion | flops 1211101184 | bytes 27820032 | tf_op jit(solution)/shard_map/bhk,btk->bht/dot_general | solution.py:21
  66.2 0.0 copy-start
  66.2 3.3 %fusion.8 = f32[64,64]{1,0:T(8,128)S(1)} fusion(f32[64,64,256]{2,1,0:T(8,128)} %get-tuple-element.6, f32[64,64]{1,0:T(8,128)S(1)} %get-tuple-element.5, pred[64,256]{1,0:T(8,128)(4,1)S(1)} %broadcast_compare_fusion), kind=kLoop, calls=%fused_computation.11 | loop fusion | flops 4190208 | bytes 4243456 | tf_op jit(solution)/shard_map/reduce_sum | solution.py:25
  69.6 0.1 copy-done
  69.7 9.0 %divide_convert_fusion = bf16[64,64,512]{2,1,0:T(8,128)(2,1)} fusion(f32[64,64]{1,0:T(8,128)S(1)} %fusion.8, bf16[64,256,576]{2,1,0:T(8,128)(2,1)} %bitcast.14, f32[64,64,256]{2,1,0:T(8,128)S(1)} %copy-done, f32[64,64]{1,0:T(8,128)S(1)} %get-tuple-element.5, pred[64,256]{1,0:T(8,128)(4,1)S(1)} %broadcast_compare_fusion), kind=kOutput, calls=%fused_computation.2 | convolution fusion | flops 1082130432 | bytes 25214976 | tf_op jit(solution)/shard_map/bht,btl->bhl/dot_general | solution.py:26
  78.6 0.1 copy.13
  78.7 0.7 reshape.86
  79.4 4.7 %all-to-all-start = ((f32[16,1,256]{2,1,0:T(1,128)}), f32[16,1,256]{2,1,0:T(1,128)S(1)}, u32[]{:S(2)}, u32[]{:S(2)}) async-start(f32[16,1,256]{2,1,0:T(1,128)} %reshape.86), calls=%async_computation | async-start | bytes 32768 | tf_op jit(solution)/shard_map/all_to_all | solution.py:31
  84.1 10.6 %fusion.22 = bf16[64,64,128]{2,0,1:T(8,128)(2,1)} fusion(bf16[64,512,128]{2,1,0:T(8,128)(2,1)} %param.7, bf16[64,64,512]{2,1,0:T(8,128)(2,1)} %divide_convert_fusion), kind=kOutput, calls=%fused_computation.19 | convolution fusion | flops 537395200 | bytes 13631488 | tf_op jit(solution)/shard_map/bhl,hlv->bhv/dot_general | solution.py:29
  94.7 0.0 all-to-all-done
  94.7 7.2 %all-to-all-start.1 = ((bf16[64,64,128]{2,0,1:T(8,128)(2,1)}), bf16[64,64,128]{2,0,1:T(8,128)(2,1)S(1)}, u32[]{:S(2)}, u32[]{:S(2)}) async-start(bf16[64,64,128]{2,0,1:T(8,128)(2,1)} %fusion.22), calls=%async_computation.1 | async-start | bytes 2097152 | tf_op jit(solution)/shard_map/all_to_all | solution.py:30
  101.9 0.5 broadcast.59
  102.4 0.7 reduce
  103.1 0.1 reshape.87
  103.3 26.6 %all-to-all-done.1 = bf16[64,64,128]{2,0,1:T(8,128)(2,1)S(1)} async-done(((bf16[64,64,128]{2,0,1:T(8,128)(2,1)}), bf16[64,64,128]{2,0,1:T(8,128)(2,1)S(1)}, u32[]{:S(2)}, u32[]{:S(2)}) %all-to-all-start.1) | async-done | bytes 1048608 | tf_op jit(solution)/shard_map/all_to_all | solution.py:30
  129.9 0.7 fusion.10
  130.6 0.7 copy.15
  (7 shorter events, 0.1 us)
Async XLA Ops:
  6.5 46.4 %all-gather.2.cloned.1.call-start = ((), (), s32[]{:S(2)}) async-start(), calls=%async_computation.2 | async-start | bytes 5570560 | tf_op jit(solution)/shard_map/all_gather | solution.py:17
  66.2 3.4 %copy-start = (f32[64,64,256]{2,1,0:T(8,128)S(1)}, f32[64,64,256]{2,1,0:T(8,128)}, u32[]{:S(2)}) copy-start(f32[64,64,256]{2,1,0:T(8,128)} %get-tuple-element.6) | copy-start | bytes 12582916
  79.4 15.3 %all-to-all-start = ((f32[16,1,256]{2,1,0:T(1,128)}), f32[16,1,256]{2,1,0:T(1,128)S(1)}, u32[]{:S(2)}, u32[]{:S(2)}) async-start(f32[16,1,256]{2,1,0:T(1,128)} %reshape.86), calls=%async_computation | async-start | bytes 32768 | tf_op jit(solution)/shard_map/all_to_all | solution.py:31
  94.7 35.2 %all-to-all-start.1 = ((bf16[64,64,128]{2,0,1:T(8,128)(2,1)}), bf16[64,64,128]{2,0,1:T(8,128)(2,1)S(1)}, u32[]{:S(2)}, u32[]{:S(2)}) async-start(bf16[64,64,128]{2,0,1:T(8,128)(2,1)} %fusion.22), calls=%async_computation.1 | async-start | bytes 2097152 | tf_op jit(solution)/shard_map/all_to_all | solution.py:30
Sparse Core Ops, SparseCore 0:
  9.0 43.9 all-gather.1
where the time goes:
time: 140 us; the launch traced here: 138 us
  waiting for transfers between devices  70.3 us (50%)
  matrix products  32.8 us (23%)
  between operations  13.5 us (10%)
  starting transfers between devices  11.9 us (8%)
  other arithmetic  5.64 us (4%)
  local copies, waits for them, and re-layouts  3.96 us (3%)
    all_gather x1, waiting for transfers between devices, local_attend(): q_all = lax.all_gather(q_own, 'dcp', axis=1, tiled=True)  43.7 us
    all_to_all x1, waiting for transfers between devices, local_attend(): v_recv = lax.all_to_all(v_part, 'dcp', 1, 1, tiled=True)  26.6 us
    dot_general x1, matrix products, local_attend(): jnp.einsum('bhk,btk->bht', q_all, c_flat, preferred_element_type=jnp.floa...  13.3 us
    dot_general x1, matrix products, local_attend(): jnp.einsum('bhl,hlv->bhv', o_part, w_uv, preferred_element_type=jnp.float32)  10.6 us
    dot_general x1, matrix products, local_attend(): jnp.einsum('bht,btl->bhl', exp_scores.astype(jnp.bfloat16), c_flat[..., :...  8.97 us
    all_to_all x1, starting transfers between devices, local_attend(): v_recv = lax.all_to_all(v_part, 'dcp', 1, 1, tiled=True)  7.23 us
    all_to_all x1, starting transfers between devices, local_attend(): lse_recv = lax.all_to_all(lse_part, 'dcp', 1, 1, tiled=True)  4.66 us
    reduce_sum x1, other arithmetic, local_attend(): row_sum = jnp.sum(exp_scores, axis=-1)  3.34 us
  transfers between devices with their start and end apart: 3, of which 2 were waited for; matrix products, arithmetic and copies ran while one was open for 9% of the time, Pallas kernels for 0%

commit v1 on v0

v1 whole, which is shorter than its diff:
```python
import functools

import jax
import jax.numpy as jnp
from jax import lax
from jax.experimental import pallas as pl
from jax.experimental.pallas import tpu as pltpu
from jax.sharding import PartitionSpec as P

MESH = pl.DeviceIdType.MESH
CHUNK_B = 8
GROUP_B = 4
UNIT_CH = 2
AHEAD = 3
LANES = 128


def kernel(dims, len_ref, q_hbm, kv_hbm, w_hbm, out_ref,
           qbuf, kvbuf, wbuf, obuf, lsebuf, vown, lown, vtw, ltw, vtr, ltr,
           va_in, la_in, vb_in, lb_in, va_out, la_out, vb_out, lb_out,
           q_sem, kv_sem, w_sem, a_send, b_send, t_send, a_recv, b_recv, t_recv,
           rt_send, rt_recv, ra_send, rb_send, ra_recv, rb_recv):
    (n_dev, head_loc, latent, rope, v_dim, pages_dev, page_len, n_batch, scale) = dims
    nz = n_dev // 2
    n_a, n_b = nz // 2, nz - 1 - nz // 2
    n_ch = n_batch // CHUNK_B
    n_unit = n_ch // UNIT_CH
    n_t = pages_dev * page_len
    n_lt = latent // LANES
    rows_ch = CHUNK_B * head_loc
    rows_g = GROUP_B * head_loc
    rows_u = rows_ch * UNIT_CH
    n_grp = CHUNK_B // GROUP_B

    me = lax.axis_index("dcp")
    z = me // 2
    c = me % 2
    sgn = 1 - 2 * c
    z_a = (z + sgn + nz) % nz
    z_b = (z - sgn + nz) % nz
    dev_a = {"dcp": z_a * 2 + c}
    dev_b = {"dcp": z_b * 2 + c}
    twin = {"dcp": z * 2 + 1 - c}

    def q_load(k):
        return pltpu.make_async_copy(q_hbm.at[k], qbuf.at[k, c, z], q_sem.at[k])

    def kv_load(k):
        part = pl.ds(k * CHUNK_B, CHUNK_B)
        return pltpu.make_async_copy(kv_hbm.at[part], kvbuf.at[part], kv_sem.at[k])

    w_load = pltpu.make_async_copy(w_hbm, wbuf, w_sem)

    for k in range(n_ch):
        q_load(k).start()

    barrier = pltpu.get_barrier_semaphore()
    for dev in (dev_a, dev_b, twin):
        pl.semaphore_signal(barrier, inc=1, device_id=dev, device_id_type=MESH)

    def remote(src, dst, send, recv, dev):
        return pltpu.make_async_remote_copy(
            src_ref=src, dst_ref=dst, send_sem=send, recv_sem=recv, device_id=dev, device_id_type=MESH)

    def q_send_a(k, slot, hop):
        ref = qbuf.at[k, c, slot]
        return remote(ref, ref, a_send, a_recv.at[k, hop], dev_a)

    def q_send_b(k, slot, hop):
        ref = qbuf.at[k, c, slot]
        return remote(ref, ref, b_send, b_recv.at[k, hop], dev_b)

    def q_send_t(k, slot):
        ref = qbuf.at[k, c, slot]
        return remote(ref, ref, t_send, t_recv.at[k], twin)

    def own_send(k):
        q_load(k).wait()
        q_send_a(k, z, 0).start()
        q_send_b(k, z, 0).start()
        q_send_t(k, z).start()

    def hop_a(k, hop):
        slot = (z - sgn * hop + nz) % nz
        q_send_a(k, slot, hop - 1).wait_recv()
        if hop < n_a:
            q_send_a(k, slot, hop).start()
        q_send_t(k, slot).start()

    def hop_b(k, hop):
        slot = (z + sgn * hop + nz) % nz
        q_send_b(k, slot, hop - 1).wait_recv()
        if hop < n_b:
            q_send_b(k, slot, hop).start()
        q_send_t(k, slot).start()

    def twin_wait(k):
        ref = qbuf.at[k, 1 - c]
        remote(ref, ref, t_send, t_recv.at[k], twin).wait_recv()

    sub8 = lax.broadcasted_iota(jnp.int32, (1, 8, 1), 1)
    first4 = sub8 < head_loc
    t_idx = lax.broadcasted_iota(jnp.int32, (1, 1, n_t), 2)
    pos = (t_idx // page_len * n_dev + me) * page_len + t_idx % page_len

    def attend(k, g):
        base = k * CHUNK_B + g * GROUP_B
        row0 = g * rows_g
        parts = []
        for j in range(n_lt):
            blk = qbuf[k, :, :, pl.ds(j * rows_ch + row0, rows_g), :]
            parts.append(blk.reshape(n_dev * rows_g, LANES))
        blk = qbuf[k, :, :, pl.ds(n_lt * rows_ch, rows_g), :]
        blk = blk.reshape(n_dev * rows_g, LANES)
        parts.append(blk[:, g * rope:(g + 1) * rope])
        lhs = jnp.concatenate(parts, axis=1)
        halves = []
        for b in range(GROUP_B):
            s = lax.dot_general(lhs, kvbuf[base + b], (((1,), (1,)), ((), ())),
                                preferred_element_type=jnp.float32)
            halves.append(s.reshape(n_dev, rows_g // 8, 8, n_t)[:, b // 2])
        outs, lses = [], []
        for p in range(GROUP_B // 2):
            b0 = base + 2 * p
            s = jnp.where(first4, halves[2 * p], halves[2 * p + 1]) * scale
            lim = jnp.where(first4, len_ref[b0], len_ref[b0 + 1])
            s = jnp.where(pos < lim, s, -jnp.inf)
            m = jnp.max(s, axis=-1, keepdims=True)
            e = jnp.exp(s - m)
            l = jnp.sum(e, axis=-1, keepdims=True)
            e0 = jnp.where(first4, e, 0.0).reshape(n_dev * 8, n_t)
            e1 = jnp.where(first4, 0.0, e).reshape(n_dev * 8, n_t)
            prob = jnp.concatenate([e0, e1], axis=1).astype(jnp.bfloat16)
            val = kvbuf[pl.ds(b0, 2), :, :latent].reshape(2 * n_t, latent)
            o = jnp.dot(prob, val, preferred_element_type=jnp.float32)
            outs.append(o.reshape(n_dev, 8, latent) / l)
            lses.append(jnp.broadcast_to(m + jnp.log(l), (n_dev, 8, LANES)))
        o = jnp.concatenate(outs, axis=1).astype(jnp.bfloat16)
        lse = jnp.concatenate(lses, axis=1)
        rows = pl.ds(pl.multiple_of((k % UNIT_CH) * rows_ch + row0, rows_g), rows_g)
        obuf[:, rows, :] = o
        lsebuf[:, rows, :] = lse

    eye = (lax.broadcasted_iota(jnp.int32, (rows_u, LANES), 0)
           == lax.broadcasted_iota(jnp.int32, (rows_u, LANES), 1))
    head_id = lax.broadcasted_iota(jnp.int32, (rows_u, 1), 0) % head_loc

    def expand(row):
        return jnp.sum(jnp.where(eye, row, 0.0), axis=1, keepdims=True)

    def project(slot, src_head):
        o = obuf[slot]
        w = jnp.concatenate([wbuf[src_head + h] for h in range(head_loc)], axis=1)
        full = jnp.dot(o, w, preferred_element_type=jnp.float32)
        v = full[:, :v_dim]
        for h in range(1, head_loc):
            v = jnp.where(head_id == h, full[:, h * v_dim:(h + 1) * v_dim], v)
        lse = jnp.sum(jnp.where(eye, lsebuf[slot], 0.0), axis=0, keepdims=True)
        return v, lse

    def twin_res(u):
        return (remote(vtw.at[u], vtr.at[u], rt_send.at[u, 0], rt_recv.at[u, 0], twin),
                remote(ltw.at[u], ltr.at[u], rt_send.at[u, 1], rt_recv.at[u, 1], twin))

    def project_unit(u):
        def other(i, _):
            v, lse = project((1 - c) * nz + i, (2 * i + 1 - c) * head_loc)
            vtw[u, i] = v
            ltw[u, pl.ds(i, 1), :] = lse
            return 0

        def own(i, _):
            v, lse = project(c * nz + i, (2 * i + c) * head_loc)
            vown[u, i] = v
            lown[u, pl.ds(i, 1), :] = lse
            return 0

        lax.fori_loop(0, nz, other, 0)
        for cp in twin_res(u):
            cp.start()
        lax.fori_loop(0, nz, own, 0)

    def weights(la, lb):
        m = jnp.maximum(la, lb)
        ea, eb = jnp.exp(la - m), jnp.exp(lb - m)
        s = ea + eb
        return ea / s, eb / s, m + jnp.log(s)

    def merge_twin(u):
        for cp in twin_res(u):
            cp.wait_recv()
        wa, wb, lse = weights(lown[u], ltr[u])
        for i in range(nz):
            vown[u, i] = expand(wa[i:i + 1]) * vown[u, i] + expand(wb[i:i + 1]) * vtr[u, i]
        lown[u] = lse

    def lse_row(u, dest):
        return lown[u, pl.ds(dest, 1), :]

    def res_a(u, hop):
        return (remote(va_out.at[u, hop], va_in.at[u, hop], ra_send.at[0], ra_recv.at[u, hop, 0], dev_a),
                remote(la_out.at[u, hop], la_in.at[u, hop], ra_send.at[1], ra_recv.at[u, hop, 1], dev_a))

    def res_b(u, hop):
        return (remote(vb_out.at[u, hop], vb_in.at[u, hop], rb_send.at[0], rb_recv.at[u, hop, 0], dev_b),
                remote(lb_out.at[u, hop], lb_in.at[u, hop], rb_send.at[1], rb_recv.at[u, hop, 1], dev_b))

    def step_dir(u, hop, n_hop, sign, res, v_in, l_in, v_out, l_out):
        dest = (z + sign * (n_hop - hop) + nz) % nz
        if hop == 0:
            v_out[u, 0] = vown[u, dest]
            l_out[u, 0] = lse_row(u, dest)
        else:
            for cp in res(u, hop - 1):
                cp.wait_recv()
            wa, wb, lse = weights(l_in[u, hop - 1], lse_row(u, dest))
            v_out[u, hop] = expand(wa) * v_in[u, hop - 1] + expand(wb) * vown[u, dest]
            l_out[u, hop] = lse
        return res(u, hop)

    def res_step(u, hop):
        cps = step_dir(u, hop, n_a, sgn, res_a, va_in, la_in, va_out, la_out)
        if hop < n_b:
            cps = cps + step_dir(u, hop, n_b, -sgn, res_b, vb_in, lb_in, vb_out, lb_out)
        for cp in cps:
            cp.start()

    def finish(u):
        for cp in res_a(u, n_a - 1) + res_b(u, n_b - 1):
            cp.wait_recv()
        wa, wb, lse = weights(la_in[u, n_a - 1], lb_in[u, n_b - 1])
        wc, wd, _ = weights(lse, lse_row(u, z))
        out = (expand(wa * wc) * va_in[u, n_a - 1] + expand(wb * wc) * vb_in[u, n_b - 1]
               + expand(wd) * vown[u, z])
        out_ref[pl.ds(pl.multiple_of(u * rows_u, rows_u), rows_u), :] = out.astype(out_ref.dtype)

    pl.semaphore_wait(barrier, 3)
    for k in range(AHEAD):
        own_send(k)
    for k in range(n_ch):
        kv_load(k).start()
    w_load.start()

    lag = (1, 3, 4, 6)
    n_round = n_ch + lag[-1]

    def when(cond, fn, *args):
        pl.when(cond)(lambda: fn(*args))

    def both(k, hop):
        def run():
            hop_a(k, hop)
            if hop <= n_b:
                hop_b(k, hop)
        pl.when((k >= 0) & (k < n_ch))(run)

    def round_body(r, _):
        both(r - lag[3], 4)
        both(r - lag[1], 2)
        when((r >= 1) & (r - 1 + AHEAD < n_ch), own_send, r - 1 + AHEAD)
        k = r - lag[3]

        def first_part():
            kv_load(k).wait()
            twin_wait(k)
            attend(k, 0)

        pl.when(k >= 0)(first_part)
        both(r - lag[2], 3)
        both(r - lag[0], 1)

        def second_part():
            for g in range(1, n_grp):
                attend(k, g)

        pl.when(k >= 0)(second_part)

        def unit_part():
            when(k == UNIT_CH - 1, w_load.wait)
            project_unit(k // UNIT_CH)

        pl.when((k >= 0) & (k % UNIT_CH == UNIT_CH - 1))(unit_part)

        def unit_merge():
            u = k // UNIT_CH - 1
            merge_twin(u)
            res_step(u, 0)

        pl.when((k >= UNIT_CH) & (k % UNIT_CH == 0))(unit_merge)
        return 0

    lax.fori_loop(1, n_round, round_body, 0)

    merge_twin(n_unit - 1)
    res_step(n_unit - 1, 0)
    for hop in range(1, n_a):
        def stage(u, _, hop=hop):
            res_step(u, hop)
            return 0
        lax.fori_loop(0, n_unit, stage, 0)

    def last(u, _):
        finish(u)
        return 0

    lax.fori_loop(0, n_unit, last, 0)

    ref = qbuf.at[:, 0, pl.ds(0, n_a)]
    remote(ref, ref, a_send, a_recv.at[0, 0], dev_a).wait_send()
    ref = qbuf.at[:, 0, pl.ds(0, n_b)]
    remote(ref, ref, b_send, b_recv.at[0, 0], dev_b).wait_send()
    ref = qbuf.at[:, 0]
    remote(ref, ref, t_send, t_recv.at[0], twin).wait_send()
    for u in range(n_unit):
        for cp in twin_res(u):
            cp.wait_send()
    remote(va_out, va_in, ra_send.at[0], ra_recv.at[0, 0, 0], dev_a).wait_send()
    remote(la_out, la_in, ra_send.at[1], ra_recv.at[0, 0, 1], dev_a).wait_send()
    remote(vb_out, vb_in, rb_send.at[0], rb_recv.at[0, 0, 0], dev_b).wait_send()
    remote(lb_out, lb_in, rb_send.at[1], rb_recv.at[0, 0, 1], dev_b).wait_send()


def solution(mesh):
    n_dev = mesh.shape["dcp"]

    def local_attend(q_own, kv_cache, lengths, w_uv):
        n_batch, pages_dev, _, page_len, kv_dim = kv_cache.shape
        head_loc = q_own.shape[1]
        latent, v_dim = w_uv.shape[1], w_uv.shape[2]
        rope = kv_dim - latent
        scale = (v_dim + rope) ** -0.5
        n_ch = n_batch // CHUNK_B
        n_unit = n_ch // UNIT_CH
        rows_ch = CHUNK_B * head_loc
        rows_u = rows_ch * UNIT_CH
        n_lt = latent // LANES
        nz = n_dev // 2
        n_a, n_b = nz // 2, nz - 1 - nz // 2
        n_grp = CHUNK_B // GROUP_B

        q = q_own.reshape(n_ch, rows_ch, kv_dim)
        lat = q[..., :latent].reshape(n_ch, rows_ch, n_lt, LANES).transpose(0, 2, 1, 3)
        lat = lat.reshape(n_ch, n_lt * rows_ch, LANES)
        rot = q[..., latent:].reshape(n_ch, n_grp, rows_ch // n_grp, rope).transpose(0, 2, 1, 3)
        rot = rot.reshape(n_ch, rows_ch // n_grp, n_grp * rope)
        q_msg = jnp.concatenate([lat, rot], axis=1)
        msg_rows = q_msg.shape[1]
        kv = kv_cache.reshape(n_batch, pages_dev * page_len, kv_dim)

        dims = (n_dev, head_loc, latent, rope, v_dim, pages_dev, page_len, n_batch, scale)
        f32, bf16 = jnp.float32, jnp.bfloat16
        dma = pltpu.SemaphoreType.DMA
        out = pl.pallas_call(
            functools.partial(kernel, dims),
            out_shape=jax.ShapeDtypeStruct((n_batch * head_loc, v_dim), bf16),
            in_specs=[
                pl.BlockSpec(memory_space=pltpu.SMEM),
                pl.BlockSpec(memory_space=pl.ANY),
                pl.BlockSpec(memory_space=pl.ANY),
                pl.BlockSpec(memory_space=pl.ANY),
            ],
            out_specs=pl.BlockSpec(memory_space=pltpu.VMEM),
            scratch_shapes=[
                pltpu.VMEM((n_ch, 2, nz, msg_rows, LANES), bf16),
                pltpu.VMEM(kv.shape, bf16),
                pltpu.VMEM(w_uv.shape, bf16),
                pltpu.VMEM((n_dev, rows_u, latent), bf16),
                pltpu.VMEM((n_dev, rows_u, LANES), f32),
                pltpu.VMEM((n_unit, nz, rows_u, v_dim), f32),
                pltpu.VMEM((n_unit, nz, LANES), f32),
                pltpu.VMEM((n_unit, nz, rows_u, v_dim), f32),
                pltpu.VMEM((n_unit, nz, LANES), f32),
                pltpu.VMEM((n_unit, nz, rows_u, v_dim), f32),
                pltpu.VMEM((n_unit, nz, LANES), f32),
                pltpu.VMEM((n_unit, n_a, rows_u, v_dim), f32),
                pltpu.VMEM((n_unit, n_a, 1, LANES), f32),
                pltpu.VMEM((n_unit, n_b, rows_u, v_dim), f32),
                pltpu.VMEM((n_unit, n_b, 1, LANES), f32),
                pltpu.VMEM((n_unit, n_a, rows_u, v_dim), f32),
                pltpu.VMEM((n_unit, n_a, 1, LANES), f32),
                pltpu.VMEM((n_unit, n_b, rows_u, v_dim), f32),
                pltpu.VMEM((n_unit, n_b, 1, LANES), f32),
                dma((n_ch,)),
                dma((n_ch,)),
                dma,
                dma,
                dma,
                dma,
                dma((n_ch, n_a)),
                dma((n_ch, n_b)),
                dma((n_ch,)),
                dma((n_unit, 2)),
                dma((n_unit, 2)),
                dma((2,)),
                dma((2,)),
                dma((n_unit, n_a, 2)),
                dma((n_unit, n_b, 2)),
            ],
            compiler_params=pltpu.CompilerParams(
                collective_id=0, has_side_effects=True, vmem_limit_bytes=60 * 1024 * 1024),
            name="mla_group",
        )(lengths, q_msg, kv, w_uv)
        return out.reshape(n_batch, head_loc, v_dim)

    return jax.shard_map(
        local_attend,
        mesh=mesh,
        in_specs=(P("dp", "dcp", None), P("dp", None, "dcp", None, None), P("dp"), P(None, None, None)),
        out_specs=P("dp", "dcp", None),
        check_vma=False,
    )
```

time: 140 us -> 79.4 us (0.57); the launches traced: 138 us -> 79.1 us
  Pallas kernels: 0 us -> 75.5 us
  waiting for transfers between devices: 70.3 us -> 0 us
  matrix products: 32.8 us -> 0 us
  between operations: 13.5 us -> 0.06 us
  starting transfers between devices: 11.9 us -> 0 us
  other arithmetic: 5.64 us -> 0.73 us
    pallas_call x0 -> x1, Pallas kernels: none -> 75.5 us  [local_attend(): pl.pallas_call(functools.partial(kernel, dims), out_shape=jax.ShapeDtypeS...]
    all_gather x1 -> x0, waiting for transfers between devices: 43.7 us -> none  [local_attend(): q_all = lax.all_gather(q_own, 'dcp', axis=1, tiled=True)]
    dot_general x3 -> x0, matrix products: 32.8 us -> none  [the longest x1 13.3 us: local_attend(): jnp.einsum('bhk,btk->bht', q_all, c_flat, preferred_element_type=jnp.floa...]
    all_to_all x2 -> x0, waiting for transfers between devices: 26.6 us -> none  [the longest x1 26.6 us: local_attend(): v_recv = lax.all_to_all(v_part, 'dcp', 1, 1, tiled=True)]
    all_to_all x2 -> x0, starting transfers between devices: 11.9 us -> none  [the longest x1 7.23 us: local_attend(): v_recv = lax.all_to_all(v_part, 'dcp', 1, 1, tiled=True)]
    reduce_sum x3 -> x0, other arithmetic: 4.07 us -> none  [the longest x1 3.34 us: local_attend(): row_sum = jnp.sum(exp_scores, axis=-1)]
  transfers between devices with their start and end apart: 3 -> 0, of which waited for: 2 -> 0; matrix products, arithmetic and copies ran while one was open for 9% -> 0% of each run, Pallas kernels for 0% -> 0%
where the time goes in v1:
time: 79.4 us; the launch traced here: 79.1 us
  Pallas kernels  75.5 us (95%)
  local copies, waits for them, and re-layouts  2.9 us (4%)
    pallas_call x1, Pallas kernels, local_attend(): pl.pallas_call(functools.partial(kernel, dims), out_shape=jax.ShapeDtypeS...  75.5 us

profile of v1, /device:TPU:22, one launch (start us, length us, event | category | flops | bytes accessed | tf_op | source)
XLA Modules:
  0.0 79.1 jit_solution(1173926763771185330)
XLA Ops:
  0.0 1.1 %reshape.21 = bf16[8,32,576]{2,1,0:T(8,128)(2,1)S(1)} reshape(bf16[64,4,576]{2,1,0:T(4,128)(2,1)} %param.4) | data formatting | bytes 589824 | tf_op jit(solution)/shard_map/reshape | solution.py:341
  1.1 0.1 copy.6
  1.2 0.1 reshape.25
  1.3 0.1 reshape.22
  1.5 0.7 pad_maximum_fusion.q_hbm
  2.2 75.5 %mla_group.1 = bf16[256,128]{1,0:T(8,128)(2,1)} custom-call(s32[64]{0:T(128)} %len_ref.1, bf16[8,144,128]{2,1,0:T(8,128)(2,1)} %pad_maximum_fusion.q_hbm, bf16[64,256,576]{2,1,0:T(8,128)(2,1)} %bitcast.7, bf16[64,512,128]{2,1,0:T(8,128)(2,1)} %w_hbm.1), custom_call_target="tpu_custom_call" | custom-call | tf_op jit(solution)/shard_map/mla_group/pallas_call | solution.py:353
  77.7 1.5 %copy.8 = bf16[64,4,128]{2,1,0:T(4,128)(2,1)} copy(bf16[64,4,128]{2,1,0:T(4,128)(2,1)} %bitcast.10) | data formatting | bytes 131072
  (3 shorter events, 0.1 us)

commit v2 on v1

--- a/solution.py
+++ b/solution.py
@@ -11,12 +11,44 @@
 CHUNK_B = 8
 GROUP_B = 4
 UNIT_CH = 2
-AHEAD = 3
 LANES = 128
+UNROLL = 4
+ORDER = (
+    (
+        ("own", 0), ("own", 1), ("own", 2), ("own", 3), ("own", 4), ("own", 5), ("hop", 0, 1), ("hop", 1, 1),
+        ("hop", 2, 1), ("hop", 4, 1), ("hop", 3, 1), ("hop", 0, 2), ("own", 6), ("hop", 1, 2), ("own", 7),
+        ("hop", 2, 2), ("hop", 0, 3), ("hop", 5, 1), ("hop", 1, 3), ("hop", 3, 2), ("hop", 4, 2), ("hop", 2, 3),
+        ("hop", 0, 4), ("hop", 5, 2), ("hop", 7, 1), ("hop", 6, 1), ("hop", 1, 4),
+    ),
+    (
+        ("hop", 3, 3), ("hop", 4, 3),
+    ),
+    (
+        ("hop", 5, 3), ("hop", 2, 4), ("hop", 6, 2), ("hop", 7, 2), ("s1", 0), ("hop", 3, 4),
+    ),
+    (
+        ("hop", 4, 4),
+    ),
+    (
+        ("hop", 6, 3), ("hop", 7, 3), ("hop", 5, 4),
+    ),
+    (
+
+    ),
+    (
+        ("hop", 6, 4), ("s1", 1), ("hop", 7, 4), ("s2", 0), ("s1", 2),
+    ),
+    (
+
+    ),
+    (
+        ("s1", 3), ("s2", 1), ("s2", 2), ("s2", 3), ("fin", 0), ("fin", 2), ("fin", 1), ("fin", 3),
+    ),
+)
 
 
 def kernel(dims, len_ref, q_hbm, kv_hbm, w_hbm, out_ref,
-           qbuf, kvbuf, wbuf, obuf, lsebuf, vown, lown, vtw, ltw, vtr, ltr,
+           qbuf, kvbuf, wbuf, obuf, lsebuf, vown, lown, lrow, wmix, vtw, ltw, vtr, ltr,
            va_in, la_in, vb_in, lb_in, va_out, la_out, vb_out, lb_out,
            q_sem, kv_sem, w_sem, a_send, b_send, t_send, a_recv, b_recv, t_recv,
            rt_send, rt_recv, ra_send, rb_send, ra_recv, rb_recv):
@@ -36,10 +68,11 @@
     z = me // 2
     c = me % 2
     sgn = 1 - 2 * c
-    z_a = (z + sgn + nz) % nz
-    z_b = (z - sgn + nz) % nz
-    dev_a = {"dcp": z_a * 2 + c}
-    dev_b = {"dcp": z_b * 2 + c}
+
+    def chip(dist):
+        return (z + sgn * dist + nz) % nz
+
+    dev_a, dev_b, dev_aa, dev_bb = ({"dcp": chip(d) * 2 + c} for d in (1, -1, 2, -2))
     twin = {"dcp": z * 2 + 1 - c}
 
     def q_load(k):
@@ -55,7 +88,7 @@
         q_load(k).start()
 
     barrier = pltpu.get_barrier_semaphore()
-    for dev in (dev_a, dev_b, twin):
+    for dev in (dev_a, dev_b, dev_aa, dev_bb, twin):
         pl.semaphore_signal(barrier, inc=1, device_id=dev, device_id_type=MESH)
 
     def remote(src, dst, send, recv, dev):
@@ -81,14 +114,14 @@
         q_send_t(k, z).start()
 
     def hop_a(k, hop):
-        slot = (z - sgn * hop + nz) % nz
+        slot = chip(-hop)
         q_send_a(k, slot, hop - 1).wait_recv()
         if hop < n_a:
             q_send_a(k, slot, hop).start()
         q_send_t(k, slot).start()
 
     def hop_b(k, hop):
-        slot = (z + sgn * hop + nz) % nz
+        slot = chip(hop)
         q_send_b(k, slot, hop - 1).wait_recv()
         if hop < n_b:
             q_send_b(k, slot, hop).start()
@@ -163,147 +196,128 @@
                 remote(ltw.at[u], ltr.at[u], rt_send.at[u, 1], rt_recv.at[u, 1], twin))
 
     def project_unit(u):
-        def other(i, _):
-            v, lse = project((1 - c) * nz + i, (2 * i + 1 - c) * head_loc)
-            vtw[u, i] = v
-            ltw[u, pl.ds(i, 1), :] = lse
-            return 0
-
-        def own(i, _):
-            v, lse = project(c * nz + i, (2 * i + c) * head_loc)
-            vown[u, i] = v
-            lown[u, pl.ds(i, 1), :] = lse
-            return 0
-
-        lax.fori_loop(0, nz, other, 0)
+        def side(cls, v_dst, l_dst):
+            def run(i, _):
+                for j in range(UNROLL):
+                    d = i * UNROLL + j
+                    v, lse = project(cls * nz + d, (2 * d + cls) * head_loc)
+                    v_dst[u, d] = v
+                    l_dst[u, pl.ds(d, 1), :] = lse
+                return 0
+
+            lax.fori_loop(0, nz // UNROLL, run, 0)
+
+        side(1 - c, vtw, ltw)
         for cp in twin_res(u):
             cp.start()
-        lax.fori_loop(0, nz, own, 0)
-
-    def weights(la, lb):
-        m = jnp.maximum(la, lb)
-        ea, eb = jnp.exp(la - m), jnp.exp(lb - m)
-        s = ea + eb
-        return ea / s, eb / s, m + jnp.log(s)
-
-    def merge_twin(u):
+        side(c, vown, lown)
+
+    def merge(terms):
+        top = functools.reduce(jnp.maximum, [l for _, l in terms])
+        es = [jnp.exp(l - top) for _, l in terms]
+        tot = functools.reduce(jnp.add, es)
+        acc = functools.reduce(jnp.add, [expand(e / tot) * v for e, (v, _) in zip(es, terms)])
+        return acc, top + jnp.log(tot)
+
+    def copies(v_src, l_src, v_dst, l_dst, u, i, send, recv, dev):
+        return (remote(v_src, v_dst.at[u, i], send.at[0], recv.at[u, i, 0], dev),
+                remote(l_src, l_dst.at[u, i], send.at[1], recv.at[u, i, 1], dev))
+
+    def send_a(u, i, v_src, l_src, dev):
+        return copies(v_src, l_src, va_in, la_in, u, i, ra_send, ra_recv, dev)
+
+    def send_b(u, i, v_src, l_src, dev):
+        return copies(v_src, l_src, vb_in, lb_in, u, i, rb_send, rb_recv, dev)
+
+    def wait_a(u, i):
+        for cp in send_a(u, i, va_out.at[u], la_out.at[u], dev_a):
+            cp.wait_recv()
+        return va_in[u, i], la_in[u, i]
+
+    def wait_b(u, i):
+        for cp in send_b(u, i, vb_out.at[u], lb_out.at[u], dev_b):
+            cp.wait_recv()
+        return vb_in[u, i], lb_in[u, i]
+
+    def stage_1(u):
         for cp in twin_res(u):
             cp.wait_recv()
-        wa, wb, lse = weights(lown[u], ltr[u])
-        for i in range(nz):
-            vown[u, i] = expand(wa[i:i + 1]) * vown[u, i] + expand(wb[i:i + 1]) * vtr[u, i]
-        lown[u] = lse
-
-    def lse_row(u, dest):
-        return lown[u, pl.ds(dest, 1), :]
-
-    def res_a(u, hop):
-        return (remote(va_out.at[u, hop], va_in.at[u, hop], ra_send.at[0], ra_recv.at[u, hop, 0], dev_a),
-                remote(la_out.at[u, hop], la_in.at[u, hop], ra_send.at[1], ra_recv.at[u, hop, 1], dev_a))
-
-    def res_b(u, hop):
-        return (remote(vb_out.at[u, hop], vb_in.at[u, hop], rb_send.at[0], rb_recv.at[u, hop, 0], dev_b),
-                remote(lb_out.at[u, hop], lb_in.at[u, hop], rb_send.at[1], rb_recv.at[u, hop, 1], dev_b))
-
-    def step_dir(u, hop, n_hop, sign, res, v_in, l_in, v_out, l_out):
-        dest = (z + sign * (n_hop - hop) + nz) % nz
-        if hop == 0:
-            v_out[u, 0] = vown[u, dest]
-            l_out[u, 0] = lse_row(u, dest)
-        else:
-            for cp in res(u, hop - 1):
-                cp.wait_recv()
-            wa, wb, lse = weights(l_in[u, hop - 1], lse_row(u, dest))
-            v_out[u, hop] = expand(wa) * v_in[u, hop - 1] + expand(wb) * vown[u, dest]
-            l_out[u, hop] = lse
-        return res(u, hop)
-
-    def res_step(u, hop):
-        cps = step_dir(u, hop, n_a, sgn, res_a, va_in, la_in, va_out, la_out)
-        if hop < n_b:
-            cps = cps + step_dir(u, hop, n_b, -sgn, res_b, vb_in, lb_in, vb_out, lb_out)
-        for cp in cps:
+        la, lb = lown[u], ltr[u]
+        top = jnp.maximum(la, lb)
+        ea, eb = jnp.exp(la - top), jnp.exp(lb - top)
+        tot = ea + eb
+        wmix[0] = ea / tot
+        wmix[1] = eb / tot
+        lown[u] = top + jnp.log(tot)
+
+        def mix(dist):
+            d = chip(dist)
+            row = pl.ds(d, 1)
+            vown[u, d] = expand(wmix[0, row, :]) * vown[u, d] + expand(wmix[1, row, :]) * vtr[u, d]
+            lrow[u, d] = lown[u, row, :]
+
+        def start(send, i, dist, dev):
+            d = chip(dist)
+            for cp in send(u, i, vown.at[u, d], lrow.at[u, d], dev):
+                cp.start()
+
+        for dist in (4, 3, -3):
+            mix(dist)
+        start(send_a, 0, 4, dev_aa)
+        start(send_a, 1, 3, dev_a)
+        start(send_b, 0, -3, dev_b)
+        for dist in (1, -1):
+            mix(dist)
+        start(send_a, 2, 1, dev_a)
+        start(send_b, 1, -1, dev_b)
+        for dist in (2, -2, 0):
+            mix(dist)
+
+    def own_term(u, dist):
+        d = chip(dist)
+        return vown[u, d], lrow[u, d]
+
+    def stage_2(u):
+        va_out[u], la_out[u] = merge([wait_a(u, 0), wait_a(u, 1), own_term(u, 2)])
+        vb_out[u], lb_out[u] = merge([wait_b(u, 0), own_term(u, -2)])
+        for cp in send_a(u, 3, va_out.at[u], la_out.at[u], dev_aa) + send_b(u, 2, vb_out.at[u], lb_out.at[u], dev_bb):
             cp.start()
 
     def finish(u):
-        for cp in res_a(u, n_a - 1) + res_b(u, n_b - 1):
-            cp.wait_recv()
-        wa, wb, lse = weights(la_in[u, n_a - 1], lb_in[u, n_b - 1])
-        wc, wd, _ = weights(lse, lse_row(u, z))
-        out = (expand(wa * wc) * va_in[u, n_a - 1] + expand(wb * wc) * vb_in[u, n_b - 1]
-               + expand(wd) * vown[u, z])
+        out, _ = merge([wait_a(u, 2), wait_b(u, 1), wait_a(u, 3), wait_b(u, 2), own_term(u, 0)])
         out_ref[pl.ds(pl.multiple_of(u * rows_u, rows_u), rows_u), :] = out.astype(out_ref.dtype)
 
-    pl.semaphore_wait(barrier, 3)
-    for k in range(AHEAD):
-        own_send(k)
+    def hop(k, h):
+        hop_a(k, h)
+        if h <= n_b:
+            hop_b(k, h)
+
+    steps = {"own": own_send, "hop": hop, "s1": stage_1, "s2": stage_2, "fin": finish}
+
+    def run_steps(r):
+        for step in ORDER[r]:
+            steps[step[0]](*step[1:])
+
+    pl.semaphore_wait(barrier, 5)
     for k in range(n_ch):
         kv_load(k).start()
     w_load.start()
 
-    lag = (1, 3, 4, 6)
-    n_round = n_ch + lag[-1]
-
-    def when(cond, fn, *args):
-        pl.when(cond)(lambda: fn(*args))
-
-    def both(k, hop):
-        def run():
-            hop_a(k, hop)
-            if hop <= n_b:
-                hop_b(k, hop)
-        pl.when((k >= 0) & (k < n_ch))(run)
-
-    def round_body(r, _):
-        both(r - lag[3], 4)
-        both(r - lag[1], 2)
-        when((r >= 1) & (r - 1 + AHEAD < n_ch), own_send, r - 1 + AHEAD)
-        k = r - lag[3]
-
-        def first_part():
-            kv_load(k).wait()
-            twin_wait(k)
-            attend(k, 0)
-
-        pl.when(k >= 0)(first_part)
-        both(r - lag[2], 3)
-        both(r - lag[0], 1)
-
-        def second_part():
-            for g in range(1, n_grp):
-                attend(k, g)
-
-        pl.when(k >= 0)(second_part)
-
-        def unit_part():
-            when(k == UNIT_CH - 1, w_load.wait)
-            project_unit(k // UNIT_CH)
-
-        pl.when((k >= 0) & (k % UNIT_CH == UNIT_CH - 1))(unit_part)
-
-        def unit_merge():
-            u = k // UNIT_CH - 1
-            merge_twin(u)
-            res_step(u, 0)
-
-        pl.when((k >= UNIT_CH) & (k % UNIT_CH == 0))(unit_merge)
+    run_steps(0)
+
+    def round_body(k, _):
+        for r in range(1, n_ch):
+            pl.when(k == r)(functools.partial(run_steps, r))
+        kv_load(k).wait()
+        twin_wait(k)
+        for g in range(n_grp):
+            attend(k, g)
+        pl.when(k == UNIT_CH - 1)(lambda: w_load.wait())
+        pl.when(k % UNIT_CH == UNIT_CH - 1)(lambda: project_unit(k // UNIT_CH))
         return 0
 
-    lax.fori_loop(1, n_round, round_body, 0)
-
-    merge_twin(n_unit - 1)
-    res_step(n_unit - 1, 0)
-    for hop in range(1, n_a):
-        def stage(u, _, hop=hop):
-            res_step(u, hop)
-            return 0
-        lax.fori_loop(0, n_unit, stage, 0)
-
-    def last(u, _):
-        finish(u)
-        return 0
-
-    lax.fori_loop(0, n_unit, last, 0)
+    lax.fori_loop(0, n_ch, round_body, 0)
+    run_steps(n_ch)
 
     ref = qbuf.at[:, 0, pl.ds(0, n_a)]
     remote(ref, ref, a_send, a_recv.at[0, 0], dev_a).wait_send()
@@ -314,10 +328,10 @@
     for u in range(n_unit):
         for cp in twin_res(u):
             cp.wait_send()
-    remote(va_out, va_in, ra_send.at[0], ra_recv.at[0, 0, 0], dev_a).wait_send()
-    remote(la_out, la_in, ra_send.at[1], ra_recv.at[0, 0, 1], dev_a).wait_send()
-    remote(vb_out, vb_in, rb_send.at[0], rb_recv.at[0, 0, 0], dev_b).wait_send()
-    remote(lb_out, lb_in, rb_send.at[1], rb_recv.at[0, 0, 1], dev_b).wait_send()
+    remote(va_in, va_in, ra_send.at[0], ra_recv.at[0, 0, 0], dev_a).wait_send()
+    remote(la_in, la_in, ra_send.at[1], ra_recv.at[0, 0, 1], dev_a).wait_send()
+    remote(vb_in, vb_in, rb_send.at[0], rb_recv.at[0, 0, 0], dev_b).wait_send()
+    remote(lb_in, lb_in, rb_send.at[1], rb_recv.at[0, 0, 1], dev_b).wait_send()
 
 
 def solution(mesh):
@@ -368,6 +382,8 @@
                 pltpu.VMEM((n_dev, rows_u, LANES), f32),
                 pltpu.VMEM((n_unit, nz, rows_u, v_dim), f32),
                 pltpu.VMEM((n_unit, nz, LANES), f32),
+                pltpu.VMEM((n_unit, nz, 1, LANES), f32),
+                pltpu.VMEM((2, nz, LANES), f32),
                 pltpu.VMEM((n_unit, nz, rows_u, v_dim), f32),
                 pltpu.VMEM((n_unit, nz, LANES), f32),
                 pltpu.VMEM((n_unit, nz, rows_u, v_dim), f32),
@@ -376,10 +392,10 @@
                 pltpu.VMEM((n_unit, n_a, 1, LANES), f32),
                 pltpu.VMEM((n_unit, n_b, rows_u, v_dim), f32),
                 pltpu.VMEM((n_unit, n_b, 1, LANES), f32),
-                pltpu.VMEM((n_unit, n_a, rows_u, v_dim), f32),
-                pltpu.VMEM((n_unit, n_a, 1, LANES), f32),
-                pltpu.VMEM((n_unit, n_b, rows_u, v_dim), f32),
-                pltpu.VMEM((n_unit, n_b, 1, LANES), f32),
+                pltpu.VMEM((n_unit, rows_u, v_dim), f32),
+                pltpu.VMEM((n_unit, 1, LANES), f32),
+                pltpu.VMEM((n_unit, rows_u, v_dim), f32),
+                pltpu.VMEM((n_unit, 1, LANES), f32),
                 dma((n_ch,)),
                 dma((n_ch,)),
                 dma,

time: 79.4 us -> 65.5 us (0.82)
  Pallas kernels: 75.5 us -> 61.6 us
    pallas_call x1, Pallas kernels: 75.5 us -> 61.6 us  [local_attend(): pl.pallas_call(functools.partial(kernel, dims), out_shape=jax.ShapeDtypeS...]
where the time goes in v2:
time: 65.5 us; the launch traced here: 65.3 us
  Pallas kernels  61.6 us (94%)
  local copies, waits for them, and re-layouts  2.9 us (4%)
  other arithmetic  0.73 us (1%)
    pallas_call x1, Pallas kernels, local_attend(): pl.pallas_call(functools.partial(kernel, dims), out_shape=jax.ShapeDtypeS...  61.6 us
    unnamed x1, local copies, waits for them, and re-layouts  1.49 us

profile of v2, /device:TPU:22, one launch (start us, length us, event | category | flops | bytes accessed | tf_op | source)
XLA Modules:
  0.0 65.3 jit_solution(9055945730079914522)
XLA Ops:
  0.0 1.1 %reshape.21 = bf16[8,32,576]{2,1,0:T(8,128)(2,1)S(1)} reshape(bf16[64,4,576]{2,1,0:T(4,128)(2,1)} %param.4) | data formatting | bytes 589824 | tf_op jit(solution)/shard_map/reshape | solution.py:355
  1.1 0.1 copy.6
  1.2 0.1 reshape.25
  1.3 0.1 reshape.22
  1.5 0.7 %pad_maximum_fusion.q_hbm = bf16[8,144,128]{2,1,0:T(8,128)(2,1)} fusion(bf16[8,16,128]{2,1,0:T(8,128)(2,1)S(1)} %reshape.25, bf16[8,128,128]{2,1,0:T(8,128)(2,1)S(1)} %bitcast.8), kind=kLoop, calls=%fused_computation | loop fusion | flops 589824 | bytes 589824 | tf_op jit(solution)/shard_map/concatenate | solution.py:360
  2.2 61.6 %mla_group.1 = bf16[256,128]{1,0:T(8,128)(2,1)} custom-call(s32[64]{0:T(128)} %len_ref.1, bf16[8,144,128]{2,1,0:T(8,128)(2,1)} %pad_maximum_fusion.q_hbm, bf16[64,256,576]{2,1,0:T(8,128)(2,1)} %bitcast.7, bf16[64,512,128]{2,1,0:T(8,128)(2,1)} %w_hbm.1), custom_call_target="tpu_custom_call" | custom-call | tf_op jit(solution)/shard_map/mla_group/pallas_call | solution.py:367
  63.8 1.5 %copy.8 = bf16[64,4,128]{2,1,0:T(4,128)(2,1)} copy(bf16[64,4,128]{2,1,0:T(4,128)(2,1)} %bitcast.10) | data formatting | bytes 131072
  (3 shorter events, 0.1 us)
